TPU v7x, 32 devices: a whole 2x2x4 slice. The times are simulated.
32 devices in a mesh: cfg: 2 (over y), ta: 4 (over z), xyz: 4 (over x, core).
Axes of the slice: x: 2, y: 2, z: 4, core: 2. Of those that a mesh axis runs over, the one named last changes fastest.
Arguments:
- sink: float32 [24, 4, 3, 2, 4, 32, 128], P('cfg', None, None, None, 'ta', 'xyz'), parts along dimension 0, may hold values from -6 to 6
- links: float32 [16, 4, 3, 3, 2, 4, 32, 128], P('cfg', None, None, None, None, 'ta', 'xyz'), parts along dimension 0, may hold values from -2 to 2
- section_index: int32 [2, 3], replicated, may hold values from 0 to 7
- momenta: int32 [33, 3], replicated, may hold values from -3 to 3
- source: int32 [3], replicated, may hold values from 0 to 15
Outputs:
- adjoint: float32 [24, 4, 3, 2, 4, 32, 128], P('cfg', None, None, None, 'ta', 'xyz'), parts along dimension 0
- correlator: float32 [4, 33, 4], P('cfg', None, 'ta'), parts along dimension 0
There are 2 independent parts, one for each index of `cfg`. A program takes and returns all parts, laid end to end along the dimension named above; an argument that names none is the same for every part. Nothing has to cross between parts.
All inputs are finite; a program needn't handle non-finite values.
Results may differ from a plain program's by a relative error of at most 0.000068.
Values sent between devices are 32-bit elements; how exact they have to be, the bound alone decides.
A program may use at most 128 MiB of HBM per device.

v0:
```python
import functools
import math

import jax
import jax.numpy as jnp
from jax import lax
from jax.experimental import pallas as pl
from jax.experimental.pallas import tpu as pltpu
from jax.sharding import PartitionSpec as P

NMOM = 33
STEPS = 2
NY = 16
NZ = 8


flow_step = 0.05


def phase_table(xcoord, nx_total, momenta, source):
    plane_index = jnp.arange(NY * NZ, dtype=jnp.int32)
    ycoord = plane_index // NZ
    zcoord = plane_index % NZ
    dist_x = jnp.mod(xcoord - source[0], nx_total)
    dist_y = jnp.mod(ycoord - source[1], NY)
    dist_z = jnp.mod(zcoord - source[2], NZ)
    frac_x = jnp.mod(momenta[:, 0:1] * dist_x[None, :], nx_total).astype(jnp.float32) / float(
        nx_total
    )
    frac_y = jnp.mod(momenta[:, 1:2] * dist_y[None, :], NY).astype(jnp.float32) / float(NY)
    frac_z = jnp.mod(momenta[:, 2:3] * dist_z[None, :], NZ).astype(jnp.float32) / float(NZ)
    frac = frac_x[:, :, None] + frac_y[:, None, :] + frac_z[:, None, :]
    angle = 2.0 * math.pi * frac
    table = jnp.concatenate([jnp.cos(angle), -jnp.sin(angle)], axis=0)
    return table.reshape(2 * NMOM, xcoord.shape[0] * NY * NZ)


MESH = pl.DeviceIdType.MESH
SECTIONS = 3 * STEPS
BLOCK = 75


def remote(src, dst, send_sem, recv_sem, axis, peer):
    return pltpu.make_async_remote_copy(
        src_ref=src, dst_ref=dst, send_sem=send_sem, recv_sem=recv_sem,
        device_id={axis: peer}, device_id_type=MESH,
    )


def multiply(link, vec, conj):
    real = imag = None
    for k in range(3):
        if conj:
            lr, li = link[k, :, 0], link[k, :, 1]
        else:
            lr, li = link[:, k, 0], link[:, k, 1]
        vr, vi = vec[k, 0][None], vec[k, 1][None]
        if conj:
            r, i = lr * vr + li * vi, lr * vi - li * vr
        else:
            r, i = lr * vr - li * vi, lr * vi + li * vr
        real = r if real is None else real + r
        imag = i if imag is None else imag + i
    return real, imag


def roll3(x, amount, axis):
    shape = x.shape
    flat = x.reshape((-1,) + shape[-2:])
    return pltpu.roll(flat, amount % flat.shape[axis], axis).reshape(shape)


def kernel(n, nx, nc, sink_ref, link_ref, table_ref, out_ref, proj_ref,
           lam, later, mixed, lk, back, hs, hr, pj,
           loc_sem, fs_sem, fr_sem, us_sem, ur_sem, ds_sem, dr_sem,
           hss_sem, hsr_sem, os_sem, or_sem, ps_sem, pr_sem):
    me = lax.axis_index("ta")
    mx = lax.axis_index("xyz")
    left, right = lax.rem(mx + nx - 1, nx), lax.rem(mx + 1, nx)
    sub = lax.broadcasted_iota(jnp.int32, (8, 128), 0)
    zc = lax.broadcasted_iota(jnp.int32, (8, 128), 1) % NZ

    barrier = pltpu.get_barrier_semaphore()
    for d in range(1, n):
        pl.semaphore_signal(barrier, inc=1, device_id={"ta": lax.rem(me + d, n)}, device_id_type=MESH)
    for d in range(1, nx):
        pl.semaphore_signal(barrier, inc=1, device_id={"xyz": lax.rem(mx + d, nx)}, device_id_type=MESH)

    own = pltpu.make_async_copy(sink_ref.at[pl.ds(me * nc, nc)], lam.at[me], loc_sem.at[SECTIONS])
    own.start()
    for s in range(SECTIONS):
        pltpu.make_async_copy(link_ref.at[s], lk.at[s, me], loc_sem.at[s]).start()
    pl.semaphore_wait(barrier, n + nx - 2)

    def field_copy(d):
        peer = lax.rem(me + d, n)
        return remote(sink_ref.at[pl.ds(peer * nc, nc)], lam.at[me],
                      fs_sem.at[d - 1], fr_sem.at[d - 1], "ta", peer)

    for d in range(1, n):
        field_copy(d).start()

    def up_copy(s, h):
        blk = lax.rem(me - h + n, n)
        return remote(lk.at[s, blk], lk.at[s, blk], us_sem.at[s, h], ur_sem.at[s, h],
                      "ta", lax.rem(me + 1, n))

    def down_copy(s, h):
        blk = lax.rem(me + h, n)
        return remote(lk.at[s, blk], lk.at[s, blk], ds_sem.at[s, h], dr_sem.at[s, h],
                      "ta", lax.rem(me + n - 1, n))

    def has_up(h):
        return jnp.logical_and(me - h >= 0, me + 1 <= n - 1)

    def has_down(h):
        return jnp.logical_and(me + h <= n - 1, me - 1 >= 0)

    def start_hop(s, h):
        @pl.when(has_up(h))
        def _():
            up_copy(s, h).start()

        @pl.when(has_down(h))
        def _():
            down_copy(s, h).start()

    def wait_hop(s, h):
        @pl.when(me - 1 - h >= 0)
        def _():
            up_copy(s, h).wait_recv()

        @pl.when(me + 1 + h <= n - 1)
        def _():
            down_copy(s, h).wait_recv()

    for s in range(SECTIONS):
        pltpu.make_async_copy(link_ref.at[s], lk.at[s, me], loc_sem.at[s]).wait()
        if s < 2:
            start_hop(s, 0)
    own.wait()
    for d in range(1, n):
        field_copy(d).wait_recv()

    def halo_copy(s, side):
        peer = (left, right)[side]
        return remote(hs.at[s % 2, side], hr.at[s % 2, side], hss_sem.at[s, side],
                      hsr_sem.at[s, side], "xyz", peer)

    def put_halo(s, t, q, value):
        hs[s % 2, 0, t, q, 0:6] = value[:, 0, :]
        hs[s % 2, 1, t, q, 0:6] = value[:, 7, :]

    def first_halo(j, carry):
        t, q = j // nc, j % nc
        put_halo(0, t, q, lam[t, q])
        return carry

    lax.fori_loop(0, n * nc, first_halo, 0)
    for side in range(2):
        halo_copy(0, side).start()

    def lap(s, source, epilogue):
        par = s % 2

        def at_time(t, carry):
            prev, following = lax.rem(t + n - 1, n), lax.rem(t + 1, n)
            ux = lk[s, t, 18:36].reshape(18, 8, 128)
            ux = roll3(ux, 1, 1)
            for j in range(18):
                row = lk[s, t, 72 + j // 8, j % 8:j % 8 + 1, :]
                back[0, j] = jnp.where(sub == 0, jnp.broadcast_to(row, (8, 128)), ux[j])
            back[1] = roll3(lk[s, t, 36:54], NZ, 2)
            uz = lk[s, t, 54:72]
            back[2] = jnp.where((zc == 0)[None], roll3(uz, 1 - NZ, 2), roll3(uz, 1, 2))

            def links(ref_block):
                return ref_block.reshape(3, 3, 2, 8, 128)

            def at_spinor(q, inner):
                v = source[t, q]
                total_r = total_i = None

                def add(acc, r, i):
                    return (r, i) if acc is None else (acc[0] + r, acc[1] + i)

                def vec(x):
                    return x.reshape(3, 2, 8, 128)

                acc = None
                r, i = multiply(links(lk[s, t, 0:18]), vec(source[following, q]), False)
                acc = add(acc, r, i)
                r, i = multiply(links(lk[s, prev, 0:18]), vec(source[prev, q]), True)
                acc = add(acc, r, i)
                high = jnp.broadcast_to(hr[par, 0, t, q, 0:6][:, None, :], (6, 8, 128))
                low = jnp.broadcast_to(hr[par, 1, t, q, 0:6][:, None, :], (6, 8, 128))
                vf = jnp.where((sub == 7)[None], high, roll3(v, -1, 1))
                r, i = multiply(links(lk[s, t, 18:36]), vec(vf), False)
                acc = add(acc, r, i)
                vb = jnp.where((sub == 0)[None], low, roll3(v, 1, 1))
                r, i = multiply(links(back[0]), vec(vb), True)
                acc = add(acc, r, i)
                r, i = multiply(links(lk[s, t, 36:54]), vec(roll3(v, -NZ, 2)), False)
                acc = add(acc, r, i)
                r, i = multiply(links(back[1]), vec(roll3(v, NZ, 2)), True)
                acc = add(acc, r, i)
                vf = jnp.where((zc == NZ - 1)[None], roll3(v, NZ - 1, 2), roll3(v, -1, 2))
                r, i = multiply(links(lk[s, t, 54:72]), vec(vf), False)
                acc = add(acc, r, i)
                vb = jnp.where((zc == 0)[None], roll3(v, 1 - NZ, 2), roll3(v, 1, 2))
                r, i = multiply(links(back[2]), vec(vb), True)
                acc = add(acc, r, i)
                hop = jnp.stack([acc[0], acc[1]], axis=1).reshape(6, 8, 128)
                nxt = epilogue(t, q, hop - 8.0 * v, v)
                put_halo(s + 1, t, q, nxt)
                return inner

            lax.fori_loop(0, nc, at_spinor, 0)
            return carry

        lax.fori_loop(0, n, at_time, 0)

    def ep_later(t, q, value, v):
        value = (0.75 * flow_step) * value
        later[t, q] = value
        return value

    def ep_middle(t, q, value, v):
        middle = lam[t, q] + (8.0 * flow_step / 9.0) * value
        lam[t, q] = middle + v
        value = (0.25 * flow_step) * middle - (2.0 * flow_step / 9.0) * v
        mixed[t, q] = value
        return value

    def ep_last(t, q, value, v):
        value = lam[t, q] + value
        lam[t, q] = value
        return value

    def step_body(i, carry):
        for k, (source, epilogue) in enumerate(((lam, ep_later), (later, ep_middle), (mixed, ep_last))):
            s = i * 3 + k
            for h in range(n - 1):
                wait_hop(s, h)
                if h < n - 2:
                    start_hop(s, h + 1)

            @pl.when(s + 2 < SECTIONS)
            def _():
                start_hop(s + 2, 0)

            for side in range(2):
                halo_copy(s, side).wait()
            lap(s, source, epilogue)

            @pl.when(s + 1 < SECTIONS)
            def _():
                for side in range(2):
                    halo_copy(s + 1, side).start()
        return carry

    lax.fori_loop(0, STEPS, step_body, 0)

    def out_copy(d):
        peer = lax.rem(me + d, n)
        return remote(lam.at[peer], out_ref.at[pl.ds(me * nc, nc)],
                      os_sem.at[d - 1], or_sem.at[d - 1], "ta", peer)

    for d in range(1, n):
        out_copy(d).start()
    out_ref[pl.ds(me * nc, nc)] = lam[me]

    for d in range(1, n):
        field_copy(d).wait_send()

    def drain(s, carry):
        for h in range(n - 1):
            @pl.when(has_up(h))
            def _():
                up_copy(s, h).wait_send()

            @pl.when(has_down(h))
            def _():
                down_copy(s, h).wait_send()
        return carry

    lax.fori_loop(0, SECTIONS, drain, 0)
    for d in range(1, n):
        out_copy(d).wait()

    def squares(j, acc):
        block = out_ref[pl.ds(j * 4, 4)]
        sq = jnp.sum(block * block, axis=1)
        return acc + ((sq[0] + sq[1]) - (sq[2] + sq[3]))

    density = lax.fori_loop(0, sink_ref.shape[0] // 4, squares, jnp.zeros((8, 128), jnp.float32))
    pj[mx] = jnp.sum(table_ref[...] * density[None], axis=1)

    def proj_copy(d):
        return remote(pj.at[mx], pj.at[mx], ps_sem.at[d - 1], pr_sem.at[d - 1],
                      "xyz", lax.rem(mx + d, nx))

    for d in range(1, nx):
        proj_copy(d).start()
    for d in range(1, nx):
        proj_copy(d).wait()
    total = pj[0]
    for j in range(1, nx):
        total = total + pj[j]
    proj_ref[...] = jnp.broadcast_to(jnp.sum(total, axis=1, keepdims=True), total.shape)


def body(n, nx, sink, links, section_index, momenta, source):
    space_cells = sink.shape[5]
    spinors = sink.shape[0] * sink.shape[1]
    nc = spinors // n
    order = jnp.concatenate([section_index[step, ::-1] for step in reversed(range(STEPS))])
    chosen = jnp.take(links, order, axis=0).reshape(SECTIONS, 72, space_cells, NY * NZ)
    rows = chosen[:, 18:36, space_cells - 1, :]
    rows = lax.ppermute(rows, "xyz", [(i, (i + 1) % nx) for i in range(nx)])
    rows = jnp.pad(rows, ((0, 0), (0, 6), (0, 0))).reshape(SECTIONS, 3, 8, NY * NZ)
    blocks = jnp.concatenate([chosen, rows], axis=1)
    nx_total = space_cells * nx
    xcoord = lax.axis_index("xyz") * space_cells + jnp.arange(space_cells, dtype=jnp.int32)
    table = phase_table(xcoord, nx_total, momenta, source)
    table = table.reshape(2 * NMOM, space_cells, NY * NZ)
    tile = (space_cells, NY * NZ)
    field = pltpu.VMEM((n, nc, 6) + tile, jnp.float32)
    dma = pltpu.SemaphoreType.DMA
    out, proj = pl.pallas_call(
        functools.partial(kernel, n, nx, nc),
        out_shape=(
            jax.ShapeDtypeStruct((spinors, 6) + tile, jnp.float32),
            jax.ShapeDtypeStruct((2 * NMOM, NY * NZ), jnp.float32),
        ),
        in_specs=[
            pl.BlockSpec(memory_space=pl.ANY),
            pl.BlockSpec(memory_space=pl.ANY),
            pl.BlockSpec(memory_space=pltpu.VMEM),
        ],
        out_specs=(pl.BlockSpec(memory_space=pltpu.VMEM), pl.BlockSpec(memory_space=pltpu.VMEM)),
        scratch_shapes=[
            field, field, field,
            pltpu.VMEM((SECTIONS, n, BLOCK) + tile, jnp.float32),
            pltpu.VMEM((3, 18) + tile, jnp.float32),
            pltpu.VMEM((2, 2, n, nc, 8, NY * NZ), jnp.float32),
            pltpu.VMEM((2, 2, n, nc, 8, NY * NZ), jnp.float32),
            pltpu.VMEM((nx, 2 * NMOM, NY * NZ), jnp.float32),
            dma((SECTIONS + 1,)),
            dma((n - 1,)), dma((n - 1,)),
            dma((SECTIONS, n - 1)), dma((SECTIONS, n - 1)),
            dma((SECTIONS, n - 1)), dma((SECTIONS, n - 1)),
            dma((SECTIONS, 2)), dma((SECTIONS, 2)),
            dma((n - 1,)), dma((n - 1,)),
            dma((nx - 1,)), dma((nx - 1,)),
        ],
        compiler_params=pltpu.CompilerParams(
            collective_id=0, has_side_effects=True, vmem_limit_bytes=60 * 1024 * 1024
        ),
    )(sink.reshape((spinors, 6) + tile), blocks, table)
    scale = 1.0 / math.sqrt(576.0 * nx_total * NY * NZ)
    correlator = (proj[:, :1] * scale).reshape(2, NMOM, 1)
    return (out.reshape(sink.shape), correlator)


def solution(mesh):
    in_specs = (
        P("cfg", None, None, None, "ta", "xyz", None),
        P("cfg", None, None, None, None, "ta", "xyz", None),
        P(),
        P(),
        P(),
    )
    out_specs = (P("cfg", None, None, None, "ta", "xyz", None), P("cfg", None, "ta"))
    step = functools.partial(body, mesh.shape["ta"], mesh.shape["xyz"])
    return jax.shard_map(step, mesh=mesh, in_specs=in_specs, out_specs=out_specs, check_vma=False)
```

profile of v0, /device:TPU:0, one launch (start us, length us, event | category | flops | bytes accessed | tf_op | source)
XLA Modules:
  0.0 208.1 jit_solution(4701151828499205393)
XLA Ops:
  0.6 0.0 copy-start
  0.6 0.8 fusion.16
  1.5 0.1 rev.7
  1.6 0.1 rev.6
  1.7 0.1 fusion.15
  1.8 0.6 copy-done
  2.3 1.9 gather_fusion
  4.2 0.1 compare_and_fusion
  4.3 1.7 broadcast_select_fusion
  6.0 1.2 copy-done.1
  7.3 0.5 collective-permute-start
  7.9 0.7 fusion.17
  8.5 0.7 and_select_fusion.2
  9.2 0.7 and_select_fusion
  9.9 0.7 and_select_fusion.4
  10.6 0.1 fusion.2
  10.6 0.1 fusion.4
  10.7 0.6 fusion
  11.3 0.7 pad_maximum_fusion.1.table_ref
  12.0 2.8 %pad_maximum_fusion.link_ref = f32[6,75,8,128]{3,2,1,0:T(8,128)} fusion(f32[6,3,8,128]{3,2,1,0:T(8,128)S(1)} %pad_bitcast_fusion, f32[6,72,8,128]{3,2,1,0:T(8,128)} %copy-done.1), kind=kLoop, calls=%fused_computation.1 | loop fusion | flops 460800 | bytes 3686400 | tf_op jit(solution)/shard_map/concatenate | solution.py:322
  14.9 189.3 %shard_map.68 = (f32[48,6,8,128]{3,2,1,0:T(8,128)}, f32[66,128]{1,0:T(8,128)}) custom-call(f32[48,6,8,128]{3,2,1,0:T(8,128)} %bitcast.29, f32[6,75,8,128]{3,2,1,0:T(8,128)} %pad_maximum_fusion.link_ref, f32[66,8,128]{2,1,0:T(8,128)} %pad_maximum_fusion.1.table_ref), custom_call_target="tpu_custom_call" | custom-call | tf_op jit(solution)/shard_map/pallas_call | solution.py:330
  204.2 0.9 multiply_reduce_fusion
  205.0 0.7 reshape.298
  205.7 2.4 %copy.15 = f32[12,4,3,2,1,8,128]{6,5,4,3,2,1,0:T(8,128)} copy(f32[12,4,3,2,1,8,128]{6,5,4,3,2,1,0:T(8,128)} %bitcast.30) | data formatting | bytes 2359296
  (11 shorter events, 0.1 us)
Async XLA Ops:
  0.6 1.7 copy-start
  4.3 3.5 %copy-start.2 = (s32[3]{0:T(128)S(1)}, s32[3]{0:T(128)}, u32[]{:S(2)}) copy-start(s32[3]{0:T(128)} %param.9) | copy-start | bytes 40
  4.3 4.9 %copy-start.3 = (s32[33,3]{0,1:T(4,128)S(1)}, s32[33,3]{0,1:T(4,128)}, u32[]{:S(2)}) copy-start(s32[33,3]{0,1:T(4,128)} %param.8) | copy-start | bytes 1192
  6.0 1.2 copy-start.1
  7.3 4.7 %collective-permute-start = (f32[6,18,128]{2,1,0:T(8,128)S(1)}, f32[6,18,128]{2,1,0:T(8,128)S(1)}, u32[]{:S(2)}, u32[]{:S(2)}) collective-permute-start(f32[6,18,128]{2,1,0:T(8,128)S(1)} %bitcast.31), channel_id=1, source_target_pairs={{0,1},{1,2},{2,3},{3,0},{4,5},{5,6},{6,7},{7,4},{8,9},{9,10},{10,1... | collective-permute-start | bytes 165896 | tf_op jit(solution)/shard_map/ppermute | solution.py:320
where the time goes:
time: 208 us
  Pallas kernels  189 us (91%)
  other arithmetic  9.04 us (4%)
  local copies, waits for them, and re-layouts  8.47 us (4%)
    pallas_call x1, Pallas kernels, body(): pl.pallas_call(functools.partial(kernel, n, nx, nc), out_shape=(jax.Shape...  189 us
    unnamed x10, local copies, waits for them, and re-layouts  4.17 us
  transfers between devices with their start and end apart: 1, of which 0 were waited for; matrix products, arithmetic and copies ran while one was open for 2% of the time, Pallas kernels for 0%

commit v1 on v0

--- a/solution.py
+++ b/solution.py
@@ -70,12 +70,15 @@
     return pltpu.roll(flat, amount % flat.shape[axis], axis).reshape(shape)
 
 
-def kernel(n, nx, nc, sink_ref, link_ref, table_ref, out_ref, proj_ref,
+def kernel(n, nx, nc, lo, hi, parts, sink_ref, link_ref, table_ref, out_ref, proj_ref,
            lam, later, mixed, lk, back, hs, hr, pj,
            loc_sem, fs_sem, fr_sem, us_sem, ur_sem, ds_sem, dr_sem,
            hss_sem, hsr_sem, os_sem, or_sem, ps_sem, pr_sem):
     me = lax.axis_index("ta")
     mx = lax.axis_index("xyz")
+    worker = jnp.logical_and(me >= lo, me < hi)
+    mine = me - lo
+    share = nc // parts
     left, right = lax.rem(mx + nx - 1, nx), lax.rem(mx + 1, nx)
     sub = lax.broadcasted_iota(jnp.int32, (8, 128), 0)
     zc = lax.broadcasted_iota(jnp.int32, (8, 128), 1) % NZ
@@ -86,19 +89,25 @@
     for d in range(1, nx):
         pl.semaphore_signal(barrier, inc=1, device_id={"xyz": lax.rem(mx + d, nx)}, device_id_type=MESH)
 
-    own = pltpu.make_async_copy(sink_ref.at[pl.ds(me * nc, nc)], lam.at[me], loc_sem.at[SECTIONS])
-    own.start()
+    def own_copy():
+        return pltpu.make_async_copy(sink_ref.at[pl.ds(mine * nc, nc)], lam.at[me], loc_sem.at[SECTIONS])
+
+    @pl.when(worker)
+    def _():
+        own_copy().start()
+
     for s in range(SECTIONS):
         pltpu.make_async_copy(link_ref.at[s], lk.at[s, me], loc_sem.at[s]).start()
     pl.semaphore_wait(barrier, n + nx - 2)
 
-    def field_copy(d):
-        peer = lax.rem(me + d, n)
-        return remote(sink_ref.at[pl.ds(peer * nc, nc)], lam.at[me],
-                      fs_sem.at[d - 1], fr_sem.at[d - 1], "ta", peer)
-
-    for d in range(1, n):
-        field_copy(d).start()
+    def field_copy(j, source):
+        return remote(sink_ref.at[pl.ds(j * nc, nc)], lam.at[source],
+                      fs_sem.at[j], fr_sem.at[source], "ta", lo + j)
+
+    for j in range(hi - lo):
+        @pl.when(me != lo + j)
+        def _():
+            field_copy(j, me).start()
 
     def up_copy(s, h):
         blk = lax.rem(me - h + n, n)
@@ -111,10 +120,10 @@
                       "ta", lax.rem(me + n - 1, n))
 
     def has_up(h):
-        return jnp.logical_and(me - h >= 0, me + 1 <= n - 1)
+        return jnp.logical_and(me - h >= 0, me + 1 <= hi - 1)
 
     def has_down(h):
-        return jnp.logical_and(me + h <= n - 1, me - 1 >= 0)
+        return jnp.logical_and(me + h <= n - 1, me - 1 >= lo)
 
     def start_hop(s, h):
         @pl.when(has_up(h))
@@ -126,11 +135,11 @@
             down_copy(s, h).start()
 
     def wait_hop(s, h):
-        @pl.when(me - 1 - h >= 0)
+        @pl.when(jnp.logical_and(me - 1 - h >= 0, me <= hi - 1))
         def _():
             up_copy(s, h).wait_recv()
 
-        @pl.when(me + 1 + h <= n - 1)
+        @pl.when(jnp.logical_and(me + 1 + h <= n - 1, me >= lo))
         def _():
             down_copy(s, h).wait_recv()
 
@@ -138,48 +147,58 @@
         pltpu.make_async_copy(link_ref.at[s], lk.at[s, me], loc_sem.at[s]).wait()
         if s < 2:
             start_hop(s, 0)
-    own.wait()
-    for d in range(1, n):
-        field_copy(d).wait_recv()
-
-    def halo_copy(s, side):
+    @pl.when(worker)
+    def _():
+        own_copy().wait()
+        for d in range(1, n):
+            field_copy(0, lax.rem(me + d, n)).wait_recv()
+
+    def halo_copy(s, side, part):
         peer = (left, right)[side]
-        return remote(hs.at[s % 2, side], hr.at[s % 2, side], hss_sem.at[s, side],
-                      hsr_sem.at[s, side], "xyz", peer)
+        return remote(hs.at[s % 2, side, part], hr.at[s % 2, side, part], hss_sem.at[s, side, part],
+                      hsr_sem.at[s, side, part], "xyz", peer)
 
     def put_halo(s, t, q, value):
-        hs[s % 2, 0, t, q, 0:6] = value[:, 0, :]
-        hs[s % 2, 1, t, q, 0:6] = value[:, 7, :]
+        hs[s % 2, 0, q // share, t, q % share, 0:6] = value[:, 0, :]
+        hs[s % 2, 1, q // share, t, q % share, 0:6] = value[:, 7, :]
 
     def first_halo(j, carry):
         t, q = j // nc, j % nc
         put_halo(0, t, q, lam[t, q])
         return carry
 
-    lax.fori_loop(0, n * nc, first_halo, 0)
-    for side in range(2):
-        halo_copy(0, side).start()
-
-    def lap(s, source, epilogue):
+    @pl.when(worker)
+    def _():
+        lax.fori_loop(0, n * nc, first_halo, 0)
+        for part in range(parts):
+            for side in range(2):
+                halo_copy(0, side, part).start()
+
+    def prepare(s):
+        def at_time(t, carry):
+            ux = roll3(lk[s, t, 18:36], 1, 1)
+            for j in range(18):
+                row = lk[s, t, 72 + j // 8, j % 8:j % 8 + 1, :]
+                back[t, 0, j] = jnp.where(sub == 0, jnp.broadcast_to(row, (8, 128)), ux[j])
+            back[t, 1] = roll3(lk[s, t, 36:54], NZ, 2)
+            uz = lk[s, t, 54:72]
+            back[t, 2] = jnp.where((zc == 0)[None], roll3(uz, 1 - NZ, 2), roll3(uz, 1, 2))
+            return carry
+
+        lax.fori_loop(0, n, at_time, 0)
+
+    def lap(s, part, source, epilogue):
         par = s % 2
 
         def at_time(t, carry):
             prev, following = lax.rem(t + n - 1, n), lax.rem(t + 1, n)
-            ux = lk[s, t, 18:36].reshape(18, 8, 128)
-            ux = roll3(ux, 1, 1)
-            for j in range(18):
-                row = lk[s, t, 72 + j // 8, j % 8:j % 8 + 1, :]
-                back[0, j] = jnp.where(sub == 0, jnp.broadcast_to(row, (8, 128)), ux[j])
-            back[1] = roll3(lk[s, t, 36:54], NZ, 2)
-            uz = lk[s, t, 54:72]
-            back[2] = jnp.where((zc == 0)[None], roll3(uz, 1 - NZ, 2), roll3(uz, 1, 2))
 
             def links(ref_block):
                 return ref_block.reshape(3, 3, 2, 8, 128)
 
-            def at_spinor(q, inner):
+            def at_spinor(w, inner):
+                q = part * share + w
                 v = source[t, q]
-                total_r = total_i = None
 
                 def add(acc, r, i):
                     return (r, i) if acc is None else (acc[0] + r, acc[1] + i)
@@ -192,30 +211,30 @@
                 acc = add(acc, r, i)
                 r, i = multiply(links(lk[s, prev, 0:18]), vec(source[prev, q]), True)
                 acc = add(acc, r, i)
-                high = jnp.broadcast_to(hr[par, 0, t, q, 0:6][:, None, :], (6, 8, 128))
-                low = jnp.broadcast_to(hr[par, 1, t, q, 0:6][:, None, :], (6, 8, 128))
+                high = jnp.broadcast_to(hr[par, 0, part, t, w, 0:6][:, None, :], (6, 8, 128))
+                low = jnp.broadcast_to(hr[par, 1, part, t, w, 0:6][:, None, :], (6, 8, 128))
                 vf = jnp.where((sub == 7)[None], high, roll3(v, -1, 1))
                 r, i = multiply(links(lk[s, t, 18:36]), vec(vf), False)
                 acc = add(acc, r, i)
                 vb = jnp.where((sub == 0)[None], low, roll3(v, 1, 1))
-                r, i = multiply(links(back[0]), vec(vb), True)
+                r, i = multiply(links(back[t, 0]), vec(vb), True)
                 acc = add(acc, r, i)
                 r, i = multiply(links(lk[s, t, 36:54]), vec(roll3(v, -NZ, 2)), False)
                 acc = add(acc, r, i)
-                r, i = multiply(links(back[1]), vec(roll3(v, NZ, 2)), True)
+                r, i = multiply(links(back[t, 1]), vec(roll3(v, NZ, 2)), True)
                 acc = add(acc, r, i)
                 vf = jnp.where((zc == NZ - 1)[None], roll3(v, NZ - 1, 2), roll3(v, -1, 2))
                 r, i = multiply(links(lk[s, t, 54:72]), vec(vf), False)
                 acc = add(acc, r, i)
                 vb = jnp.where((zc == 0)[None], roll3(v, 1 - NZ, 2), roll3(v, 1, 2))
-                r, i = multiply(links(back[2]), vec(vb), True)
+                r, i = multiply(links(back[t, 2]), vec(vb), True)
                 acc = add(acc, r, i)
                 hop = jnp.stack([acc[0], acc[1]], axis=1).reshape(6, 8, 128)
                 nxt = epilogue(t, q, hop - 8.0 * v, v)
                 put_halo(s + 1, t, q, nxt)
                 return inner
 
-            lax.fori_loop(0, nc, at_spinor, 0)
+            lax.fori_loop(0, share, at_spinor, 0)
             return carry
 
         lax.fori_loop(0, n, at_time, 0)
@@ -237,44 +256,69 @@
         lam[t, q] = value
         return value
 
+    def out_copy(t, part, j):
+        return remote(lam.at[t, pl.ds(part * share, share)],
+                      out_ref.at[pl.ds(j * nc + part * share, share)],
+                      os_sem.at[t, part], or_sem.at[j, part], "ta", t)
+
+    hops = hi - 1
+
+    def pass_on(s):
+        for h in range(hops - 1):
+            wait_hop(s, h)
+            start_hop(s, h + 1)
+
+    pass_on(0)
+
     def step_body(i, carry):
         for k, (source, epilogue) in enumerate(((lam, ep_later), (later, ep_middle), (mixed, ep_last))):
             s = i * 3 + k
-            for h in range(n - 1):
-                wait_hop(s, h)
-                if h < n - 2:
-                    start_hop(s, h + 1)
+            @pl.when(s + 1 < SECTIONS)
+            def _():
+                pass_on(s + 1)
 
             @pl.when(s + 2 < SECTIONS)
             def _():
                 start_hop(s + 2, 0)
 
-            for side in range(2):
-                halo_copy(s, side).wait()
-            lap(s, source, epilogue)
-
-            @pl.when(s + 1 < SECTIONS)
+            wait_hop(s, hops - 1)
+
+            @pl.when(worker)
             def _():
-                for side in range(2):
-                    halo_copy(s + 1, side).start()
+                prepare(s)
+
+                def at_part(part, inner):
+                    for side in range(2):
+                        halo_copy(s, side, part).wait()
+                    lap(s, part, source, epilogue)
+
+                    @pl.when(s + 1 < SECTIONS)
+                    def _():
+                        for side in range(2):
+                            halo_copy(s + 1, side, part).start()
+
+                    @pl.when(s + 1 == SECTIONS)
+                    def _():
+                        for d in range(1, n):
+                            out_copy(lax.rem(me + d, n), part, mine).start()
+                    return inner
+
+                lax.fori_loop(0, parts, at_part, 0)
         return carry
 
     lax.fori_loop(0, STEPS, step_body, 0)
 
-    def out_copy(d):
-        peer = lax.rem(me + d, n)
-        return remote(lam.at[peer], out_ref.at[pl.ds(me * nc, nc)],
-                      os_sem.at[d - 1], or_sem.at[d - 1], "ta", peer)
-
-    for d in range(1, n):
-        out_copy(d).start()
-    out_ref[pl.ds(me * nc, nc)] = lam[me]
-
-    for d in range(1, n):
-        field_copy(d).wait_send()
+    @pl.when(worker)
+    def _():
+        out_ref[pl.ds(mine * nc, nc)] = lam[me]
+
+    for j in range(hi - lo):
+        @pl.when(me != lo + j)
+        def _():
+            field_copy(j, me).wait_send()
 
     def drain(s, carry):
-        for h in range(n - 1):
+        for h in range(hops):
             @pl.when(has_up(h))
             def _():
                 up_copy(s, h).wait_send()
@@ -285,8 +329,17 @@
         return carry
 
     lax.fori_loop(0, SECTIONS, drain, 0)
-    for d in range(1, n):
-        out_copy(d).wait()
+    @pl.when(worker)
+    def _():
+        for part in range(parts):
+            for d in range(1, n):
+                out_copy(lax.rem(me + d, n), part, mine).wait_send()
+
+    for j in range(hi - lo):
+        @pl.when(me != lo + j)
+        def _():
+            for part in range(parts):
+                out_copy(lo + j, part, j).wait_recv()
 
     def squares(j, acc):
         block = out_ref[pl.ds(j * 4, 4)]
@@ -313,7 +366,10 @@
 def body(n, nx, sink, links, section_index, momenta, source):
     space_cells = sink.shape[5]
     spinors = sink.shape[0] * sink.shape[1]
-    nc = spinors // n
+    lo = n // 4 if spinors % (n - 2 * (n // 4)) == 0 else 0
+    hi = n - lo
+    nc = spinors // (hi - lo)
+    parts = 3 if nc % 3 == 0 else 1
     order = jnp.concatenate([section_index[step, ::-1] for step in reversed(range(STEPS))])
     chosen = jnp.take(links, order, axis=0).reshape(SECTIONS, 72, space_cells, NY * NZ)
     rows = chosen[:, 18:36, space_cells - 1, :]
@@ -328,7 +384,7 @@
     field = pltpu.VMEM((n, nc, 6) + tile, jnp.float32)
     dma = pltpu.SemaphoreType.DMA
     out, proj = pl.pallas_call(
-        functools.partial(kernel, n, nx, nc),
+        functools.partial(kernel, n, nx, nc, lo, hi, parts),
         out_shape=(
             jax.ShapeDtypeStruct((spinors, 6) + tile, jnp.float32),
             jax.ShapeDtypeStruct((2 * NMOM, NY * NZ), jnp.float32),
@@ -342,16 +398,16 @@
         scratch_shapes=[
             field, field, field,
             pltpu.VMEM((SECTIONS, n, BLOCK) + tile, jnp.float32),
-            pltpu.VMEM((3, 18) + tile, jnp.float32),
-            pltpu.VMEM((2, 2, n, nc, 8, NY * NZ), jnp.float32),
-            pltpu.VMEM((2, 2, n, nc, 8, NY * NZ), jnp.float32),
+            pltpu.VMEM((n, 3, 18) + tile, jnp.float32),
+            pltpu.VMEM((2, 2, parts, n, nc // parts, 8, NY * NZ), jnp.float32),
+            pltpu.VMEM((2, 2, parts, n, nc // parts, 8, NY * NZ), jnp.float32),
             pltpu.VMEM((nx, 2 * NMOM, NY * NZ), jnp.float32),
             dma((SECTIONS + 1,)),
-            dma((n - 1,)), dma((n - 1,)),
+            dma((hi - lo,)), dma((n,)),
             dma((SECTIONS, n - 1)), dma((SECTIONS, n - 1)),
             dma((SECTIONS, n - 1)), dma((SECTIONS, n - 1)),
-            dma((SECTIONS, 2)), dma((SECTIONS, 2)),
-            dma((n - 1,)), dma((n - 1,)),
+            dma((SECTIONS, 2, parts)), dma((SECTIONS, 2, parts)),
+            dma((n, parts)), dma((hi - lo, parts)),
             dma((nx - 1,)), dma((nx - 1,)),
         ],
         compiler_params=pltpu.CompilerParams(

time: 208 us -> 178 us (0.86)
  Pallas kernels: 189 us -> 159 us
    pallas_call x1, Pallas kernels: 189 us -> 159 us  [body(): pl.pallas_call(functools.partial(kernel, n, nx, nc, lo, hi, parts), out_s...]
where the time goes in v1:
time: 178 us
  Pallas kernels  159 us (89%)
  other arithmetic  9.04 us (5%)
  local copies, waits for them, and re-layouts  8.47 us (5%)
    pallas_call x1, Pallas kernels, body(): pl.pallas_call(functools.partial(kernel, n, nx, nc, lo, hi, parts), out_s...  159 us
    unnamed x10, local copies, waits for them, and re-layouts  4.17 us
  transfers between devices with their start and end apart: 1, of which 0 were waited for; matrix products, arithmetic and copies ran while one was open for 2% of the time, Pallas kernels for 0%

profile of v1, /device:TPU:0, one launch (start us, length us, event | category | flops | bytes accessed | tf_op | source)
XLA Modules:
  0.0 177.7 jit_solution(9229025121455817402)
XLA Ops:
  0.6 0.0 copy-start
  0.6 0.8 fusion.16
  1.5 0.1 rev.7
  1.6 0.1 rev.6
  1.7 0.1 fusion.15
  1.8 0.6 copy-done
  2.3 1.9 %gather_fusion = f32[6,4,3,3,2,8,128]{6,5,4,3,2,1,0:T(8,128)} fusion(f32[8,4,3,3,2,8,128]{6,5,4,3,2,1,0:T(8,128)S(1)} %bitcast.27, s32[1024]{0:T(1024)S(1)} %pad_clamp_fusion), kind=kCustom, calls=%fused_computation | custom fusion | bytes 3538968 | tf_op jit(solution)/shard_map/jit(_take)/gather | solution.py:374
  4.2 0.1 compare_and_fusion
  4.3 1.7 broadcast_select_fusion
  6.0 1.2 copy-done.1
  7.3 0.5 collective-permute-start
  7.9 0.7 fusion.17
  8.5 0.7 and_select_fusion.2
  9.2 0.7 and_select_fusion
  9.9 0.7 and_select_fusion.4
  10.6 0.1 fusion.2
  10.6 0.1 fusion.4
  10.7 0.6 fusion
  11.3 0.7 pad_maximum_fusion.1.table_ref
  12.0 2.8 %pad_maximum_fusion.link_ref = f32[6,75,8,128]{3,2,1,0:T(8,128)} fusion(f32[6,3,8,128]{3,2,1,0:T(8,128)S(1)} %pad_bitcast_fusion, f32[6,72,8,128]{3,2,1,0:T(8,128)} %copy-done.1), kind=kLoop, calls=%fused_computation.1 | loop fusion | flops 460800 | bytes 3686400 | tf_op jit(solution)/shard_map/concatenate | solution.py:378
  14.9 158.9 %shard_map.68 = (f32[48,6,8,128]{3,2,1,0:T(8,128)}, f32[66,128]{1,0:T(8,128)}) custom-call(f32[48,6,8,128]{3,2,1,0:T(8,128)} %bitcast.29, f32[6,75,8,128]{3,2,1,0:T(8,128)} %pad_maximum_fusion.link_ref, f32[66,8,128]{2,1,0:T(8,128)} %pad_maximum_fusion.1.table_ref), custom_call_target="tpu_custom_call" | custom-call | tf_op jit(solution)/shard_map/pallas_call | solution.py:386
  173.8 0.9 multiply_reduce_fusion
  174.7 0.7 reshape.298
  175.4 2.4 %copy.15 = f32[12,4,3,2,1,8,128]{6,5,4,3,2,1,0:T(8,128)} copy(f32[12,4,3,2,1,8,128]{6,5,4,3,2,1,0:T(8,128)} %bitcast.30) | data formatting | bytes 2359296
  (11 shorter events, 0.1 us)
Async XLA Ops:
  0.6 1.7 copy-start
  4.3 3.5 %copy-start.2 = (s32[3]{0:T(128)S(1)}, s32[3]{0:T(128)}, u32[]{:S(2)}) copy-start(s32[3]{0:T(128)} %param.9) | copy-start | bytes 40
  4.3 4.9 %copy-start.3 = (s32[33,3]{0,1:T(4,128)S(1)}, s32[33,3]{0,1:T(4,128)}, u32[]{:S(2)}) copy-start(s32[33,3]{0,1:T(4,128)} %param.8) | copy-start | bytes 1192
  6.0 1.2 copy-start.1
  7.3 4.7 %collective-permute-start = (f32[6,18,128]{2,1,0:T(8,128)S(1)}, f32[6,18,128]{2,1,0:T(8,128)S(1)}, u32[]{:S(2)}, u32[]{:S(2)}) collective-permute-start(f32[6,18,128]{2,1,0:T(8,128)S(1)} %bitcast.31), channel_id=1, source_target_pairs={{0,1},{1,2},{2,3},{3,0},{4,5},{5,6},{6,7},{7,4},{8,9},{9,10},{10,1... | collective-permute-start | bytes 165896 | tf_op jit(solution)/shard_map/ppermute | solution.py:376
